TPU v7x, 128 devices: a whole 4x4x4 slice. The times are simulated.
128 devices in a mesh: farcp: 2 (over x_lo), nearcp: 8 (over z_hi, x_hi, core), model: 8 (over z_lo, y).
Axes of the slice: x: 4 (x_hi: 2, x_lo: 2; x = x_hi * 2 + x_lo), y: 4, z: 4 (z_hi: 2, z_lo: 2; z = z_hi * 2 + z_lo), core: 2. Of those that a mesh axis runs over, the one named last changes fastest.
Arguments:
- raw_keys: bfloat16 [16, 16384, 8, 128], P(None, ('farcp', 'nearcp'), 'model'), may hold values from -6 to 6
- raw_values: bfloat16 [16, 16384, 8, 128], P(None, ('farcp', 'nearcp'), 'model'), may hold values from -6 to 6
- turn_angle: float32 [16384, 64], replicated, may hold values from -3.140625 to 3.140625
- key_gain: float32 [128], replicated, may hold values from 0.25 to 1.75
Outputs:
- stored_keys: bfloat16 [16, 16384, 8, 128], P(('farcp', 'nearcp'), None, 'model')
- stored_values: bfloat16 [16, 16384, 8, 128], P(('farcp', 'nearcp'), None, 'model')
- key_scale: float32 [16, 8, 128], P(('farcp', 'nearcp'), 'model')
All inputs are finite; a program needn't handle non-finite values. Where the computation divides by a largest or mean magnitude, that divisor is 1e-20 or more.
Results may differ from a plain program's by a relative error of at most 0.001.
Values may be sent and summed in bfloat16 or wider, within the bound.
A program may use at most 192 MiB of HBM per device.

v0:
```python
import jax
import jax.numpy as jnp
from jax import lax
from jax.sharding import PartitionSpec as P


def apply_rotary(vectors, angle):
    half = vectors.shape[-1] // 2
    cosine, sine = (jnp.cos(angle)[None, :, None, :], jnp.sin(angle)[None, :, None, :])
    first, second = (vectors[..., :half], vectors[..., half:])
    return jnp.concatenate(
        [first * cosine - second * sine, second * cosine + first * sine], axis=-1
    )


def scale_rows(vectors, row_gain):
    return (
        vectors * lax.rsqrt(jnp.mean(vectors * vectors, axis=-1, keepdims=True) + 1e-06) * row_gain
    )


def prepare_keys(plain_keys, angle, key_gain):
    wide_keys = plain_keys.astype(jnp.float32)
    wide_keys = scale_rows(wide_keys, key_gain)
    return apply_rotary(wide_keys, angle)


def local(raw_keys, raw_values, turn_angle, key_gain):
    moved_keys, stored_values = (
        lax.all_to_all(raw_keys, ("farcp", "nearcp"), split_axis=0, concat_axis=1, tiled=True),
        lax.all_to_all(raw_values, ("farcp", "nearcp"), split_axis=0, concat_axis=1, tiled=True),
    )
    turned_keys = prepare_keys(moved_keys, turn_angle, key_gain)
    key_scale = jnp.max(jnp.abs(turned_keys), axis=1)
    narrow_keys = (turned_keys / key_scale[:, None]).astype(jnp.bfloat16)
    return (narrow_keys, stored_values, key_scale)


def solution(mesh):
    in_specs = (
        P(None, ("farcp", "nearcp"), "model", None),
        P(None, ("farcp", "nearcp"), "model", None),
        P(),
        P(),
    )
    out_specs = (
        P(("farcp", "nearcp"), None, "model", None),
        P(("farcp", "nearcp"), None, "model", None),
        P(("farcp", "nearcp"), "model", None),
    )
    return jax.shard_map(local, mesh=mesh, in_specs=in_specs, out_specs=out_specs, check_vma=False)
```

profile of v0, /device:TPU:1, one launch (start us, length us, event | category | flops | bytes accessed | tf_op | source)
XLA Modules:
  0.0 129.9 jit_solution(10801401433687837809)
XLA Ops:
  0.6 9.1 %all-to-all-start = ((bf16[16,1024,1,128]{3,1,2,0:T(8,128)(2,1)}), bf16[16,1024,1,128]{3,1,2,0:T(8,128)(2,1)}, u32[]{:S(2)}, u32[]{:S(2)}) async-start(bf16[16,1024,1,128]{3,1,2,0:T(8,128)(2,1)} %param.4), calls=%async_computation | async-start | bytes 8388608 | tf_op jit(solution)/shard_map/all_to_all | solution.py:30
  9.8 6.9 %copy.7 = f32[16384,64]{1,0:T(8,128)} copy(f32[16384,64]{0,1:T(8,128)} %param.6) | data formatting | bytes 8388608 | tf_op args[2]
  16.6 31.5 %fusion.2 = (f32[16384,64]{1,0:T(8,128)}, f32[16384,64]{1,0:T(8,128)}) fusion(f32[16384,64]{1,0:T(8,128)} %copy.7), kind=kLoop, calls=%fused_computation.12 | loop fusion | bytes 12582912 | tf_op jit(solution)/shard_map/cos | solution.py:9
  48.1 0.0 copy-start.3
  48.2 15.4 %all-to-all-done = bf16[16,1024,1,128]{3,1,2,0:T(8,128)(2,1)} async-done(((bf16[16,1024,1,128]{3,1,2,0:T(8,128)(2,1)}), bf16[16,1024,1,128]{3,1,2,0:T(8,128)(2,1)}, u32[]{:S(2)}, u32[]{:S(2)}) %all-to-all-start) | async-done | bytes 4194336 | tf_op jit(solution)/shard_map/all_to_all | solution.py:30
  63.5 8.8 %all-to-all-start.1 = ((bf16[16,1024,1,128]{3,1,2,0:T(8,128)(2,1)}), bf16[16,1024,1,128]{3,1,2,0:T(8,128)(2,1)}, u32[]{:S(2)}, u32[]{:S(2)}) async-start(bf16[16,1024,1,128]{3,1,2,0:T(8,128)(2,1)} %param.5), calls=%async_computation.1 | async-start | bytes 8388608 | tf_op jit(solution)/shard_map/all_to_all | solution.py:31
  72.4 4.4 %multiply_reduce_fusion = f32[16,1024]{1,0:T(8,128)S(1)} fusion(bf16[16,1024,1,128]{3,1,2,0:T(8,128)(2,1)} %all-to-all-done), kind=kLoop, calls=%fused_computation.10 | loop fusion | flops 6275072 | bytes 4259840 | tf_op jit(solution)/shard_map/reduce_sum | solution.py:18
  76.9 0.0 copy-done.3
  76.9 9.9 %multiply_multiply_fusion = f32[1,16384,1,128]{3,1,2,0:T(8,128)} fusion(f32[128]{0:T(128)S(1)} %copy-done.3, f32[16384]{0:T(1024)S(1)} %bitcast.21, bf16[1,16384,1,128]{3,1,2,0:T(8,128)(2,1)} %bitcast.20), kind=kLoop, calls=%fused_computation.9 | loop fusion | flops 6291456 | bytes 12648960 | tf_op jit(solution)/shard_map/mul | solution.py:18
  86.8 17.3 %fusion = (f32[1,16384,1,64]{3,1,2,0:T(8,128)}, f32[1,16384,1,64]{3,1,2,0:T(8,128)}) fusion(f32[16384,64]{1,0:T(8,128)} %get-tuple-element.6, f32[16384,64]{1,0:T(8,128)} %get-tuple-element.5, f32[1,16384,1,128]{3,1,2,0:T(8,128)} %multiply_multiply_fusion), kind=kLoop, calls=%fused_computation.3 | loop fusion | flops 6291456 | bytes 25165824 | tf_op jit(solution)/shard_map/sub | solution.py:12
  104.1 0.0 copy-start
  104.1 0.0 copy-start.1
  104.1 7.7 %abs_reduce_fusion = f32[128]{0:T(128)S(1)} fusion(f32[1,16384,1,64]{3,1,2,0:T(8,128)} %get-tuple-element.4, f32[1,16384,1,64]{3,1,2,0:T(8,128)} %get-tuple-element.3), kind=kLoop, calls=%fused_computation.8 | loop fusion | flops 6291328 | bytes 8389120 | tf_op jit(solution)/shard_map/reduce_max | solution.py:34
  111.8 0.5 copy-done
  112.3 2.4 %copy-done.1 = f32[1,16384,1,64]{3,1,2,0:T(8,128)S(1)} copy-done((f32[1,16384,1,64]{3,1,2,0:T(8,128)S(1)}, f32[1,16384,1,64]{3,1,2,0:T(8,128)}, u32[]{:S(2)}) %copy-start.1) | copy-done | bytes 4194328
  114.7 0.0 copy-start.2
  114.7 3.6 %divide_convert_fusion = bf16[1,16384,1,128]{3,1,2,0:T(8,128)(2,1)} fusion(f32[128]{0:T(128)S(1)} %abs_reduce_fusion, f32[1,16384,1,64]{3,1,2,0:T(8,128)S(1)} %copy-done.1, f32[1,16384,1,64]{3,1,2,0:T(8,128)S(1)} %copy-done), kind=kLoop, calls=%fused_computation.7 | loop fusion | flops 6291456 | bytes 12583424 | tf_op jit(solution)/shard_map/convert_element_type | solution.py:35
  118.4 0.0 copy-done.2
  118.4 7.8 %all-to-all-done.1 = bf16[16,1024,1,128]{3,1,2,0:T(8,128)(2,1)} async-done(((bf16[16,1024,1,128]{3,1,2,0:T(8,128)(2,1)}), bf16[16,1024,1,128]{3,1,2,0:T(8,128)(2,1)}, u32[]{:S(2)}, u32[]{:S(2)}) %all-to-all-start.1) | async-done | bytes 4194336 | tf_op jit(solution)/shard_map/all_to_all | solution.py:31
  126.2 3.7 %copy.11 = bf16[1,16384,1,128]{3,1,2,0:T(8,128)(2,1)} copy(bf16[1,16384,1,128]{3,1,2,0:T(8,128)(2,1)} %bitcast.3) | data formatting | bytes 8388608
  (2 shorter events, 0.0 us)
Async XLA Ops:
  0.6 62.9 %all-to-all-start = ((bf16[16,1024,1,128]{3,1,2,0:T(8,128)(2,1)}), bf16[16,1024,1,128]{3,1,2,0:T(8,128)(2,1)}, u32[]{:S(2)}, u32[]{:S(2)}) async-start(bf16[16,1024,1,128]{3,1,2,0:T(8,128)(2,1)} %param.4), calls=%async_computation | async-start | bytes 8388608 | tf_op jit(solution)/shard_map/all_to_all | solution.py:30
  48.1 28.7 %copy-start.3 = (f32[128]{0:T(128)S(1)}, f32[128]{0:T(128)}, u32[]{:S(2)}) copy-start(f32[128]{0:T(128)} %param.7) | copy-start | bytes 1540
  63.5 62.6 %all-to-all-start.1 = ((bf16[16,1024,1,128]{3,1,2,0:T(8,128)(2,1)}), bf16[16,1024,1,128]{3,1,2,0:T(8,128)(2,1)}, u32[]{:S(2)}, u32[]{:S(2)}) async-start(bf16[16,1024,1,128]{3,1,2,0:T(8,128)(2,1)} %param.5), calls=%async_computation.1 | async-start | bytes 8388608 | tf_op jit(solution)/shard_map/all_to_all | solution.py:31
  104.1 8.2 %copy-start = (f32[1,16384,1,64]{3,1,2,0:T(8,128)S(1)}, f32[1,16384,1,64]{3,1,2,0:T(8,128)}, u32[]{:S(2)}) copy-start(f32[1,16384,1,64]{3,1,2,0:T(8,128)} %get-tuple-element.3) | copy-start | bytes 12582916
  104.1 10.6 %copy-start.1 = (f32[1,16384,1,64]{3,1,2,0:T(8,128)S(1)}, f32[1,16384,1,64]{3,1,2,0:T(8,128)}, u32[]{:S(2)}) copy-start(f32[1,16384,1,64]{3,1,2,0:T(8,128)} %get-tuple-element.4) | copy-start | bytes 12582916
  114.7 3.6 %copy-start.2 = (f32[128]{0:T(128)}, f32[128]{0:T(128)S(1)}, u32[]{:S(2)}) copy-start(f32[128]{0:T(128)S(1)} %abs_reduce_fusion) | copy-start | bytes 1540
where the time goes:
time: 132 us; the launch traced here: 130 us
  local copies, waits for them, and re-layouts  45 us (34%)
  other arithmetic  43 us (33%)
  waiting for transfers between devices  23.2 us (18%)
  starting transfers between devices  18 us (14%)
    cos x1, local copies, waits for them, and re-layouts, apply_rotary(): jnp.cos(angle)[None, :, None, :]  31.5 us
    sub x1, other arithmetic, apply_rotary(): first * cosine - second * sine  17.3 us
    all_to_all x1, waiting for transfers between devices, local(): lax.all_to_all(raw_keys, ('farcp', 'nearcp'), split_axis=0, concat_axis=1...  15.4 us
    unnamed x11, local copies, waits for them, and re-layouts  13.5 us
    mul x1, other arithmetic, scale_rows(): vectors * lax.rsqrt(jnp.mean(vectors * vectors, axis=-1, keepdims=True) +...  9.9 us
    all_to_all x1, starting transfers between devices, local(): lax.all_to_all(raw_keys, ('farcp', 'nearcp'), split_axis=0, concat_axis=1...  9.13 us
    all_to_all x1, starting transfers between devices, local(): lax.all_to_all(raw_values, ('farcp', 'nearcp'), split_axis=0, concat_axis...  8.84 us
    all_to_all x1, waiting for transfers between devices, local(): lax.all_to_all(raw_values, ('farcp', 'nearcp'), split_axis=0, concat_axis...  7.8 us
  transfers between devices with their start and end apart: 2, of which 2 were waited for; matrix products, arithmetic and copies ran while one was open for 63% of the time, Pallas kernels for 0%

commit v1 on v0

v1 whole, which is shorter than its diff:
```python
import jax
import jax.numpy as jnp
from jax import lax
from jax.experimental import pallas as pl
from jax.experimental.pallas import tpu as pltpu
from jax.sharding import PartitionSpec as P

MESH = pl.DeviceIdType.MESH
SEQS, ROWS, LANES, HALF = 16, 1024, 128, 64
TOTAL = SEQS * ROWS
CHUNK = 128
FIRST_ROWS = 512


def interleave(a, b):
    merged = []
    for i in range(max(len(a), len(b))):
        merged += a[i : i + 1] + b[i : i + 1]
    return merged


ALONG_Z = [(0, 1, c) for c in (0, 1)]
ALONG_X = [(dx, 0, c) for c in (0, 1) for dx in (1, 3, 2)]
DIAGONAL = [(dx, 1, c) for c in (0, 1) for dx in (1, 3, 2)]
ORDER = interleave(ALONG_Z + DIAGONAL, ALONG_X) + [(0, 0, 1)]
PEERS = len(ORDER)


def exchange(
    keys, values, angle, gain,
    kland, vland, scale,
    raw, turned, narrow, angles, gains_row, cosines, sines, maxes,
    local_sem, v_send, v_recv, k_send, k_recv, m_send, m_recv,
):
    far, near, model = lax.axis_index("farcp"), lax.axis_index("nearcp"), lax.axis_index("model")
    core, x, z = near % 2, ((near // 2) % 2) * 2 + far, near // 4
    me = far * 8 + near

    def place(dx, dz, dc):
        px, pz, pc = (x + dx) % 4, (z + dz) % 2, (core + dc) % 2
        return px % 2, pz * 4 + (px // 2) * 2 + pc

    peers = [place(*step) for step in ORDER]
    ids = [(f, n, model) for f, n in peers]
    index = [f * 8 + n for f, n in peers]

    load_keys = pltpu.make_async_copy(keys, raw, local_sem.at[0])
    load_angles = pltpu.make_async_copy(
        angle.at[:, pl.ds(pl.multiple_of(me * ROWS, ROWS), ROWS)], angles, local_sem.at[1]
    )
    keep = pltpu.make_async_copy(
        values.at[me], vland.at[pl.ds(pl.multiple_of(me * ROWS, ROWS), ROWS)], local_sem.at[2]
    )
    load_keys.start()
    load_angles.start()
    load_gain = pltpu.make_async_copy(gain, gains_row, local_sem.at[3])
    load_gain.start()

    barrier = pltpu.get_barrier_semaphore()
    for device in ids:
        pl.semaphore_signal(barrier, inc=1, device_id=device, device_id_type=MESH)
    pl.semaphore_wait(barrier, PEERS)

    def send_values(part, first, rows):
        copies = [
            pltpu.make_async_remote_copy(
                src_ref=values.at[index[i], pl.ds(first, rows)],
                dst_ref=vland.at[pl.ds(pl.multiple_of(me * ROWS + first, CHUNK), rows)],
                send_sem=v_send.at[part, i],
                recv_sem=v_recv.at[part, i],
                device_id=ids[i],
                device_id_type=MESH,
            )
            for i in range(PEERS)
        ]
        for copy in copies:
            copy.start()
        return copies

    copies = send_values(0, 0, FIRST_ROWS)
    keep.start()

    load_angles.wait()
    for c in range(ROWS // CHUNK):
        a = angles[:, c * CHUNK : (c + 1) * CHUNK]
        cosine, sine = jnp.cos(a), jnp.sin(a)
        rows = pl.ds(c * CHUNK, CHUNK)
        cosines[rows, :] = jnp.concatenate([cosine, cosine], axis=0).T
        sines[rows, :] = jnp.concatenate([-sine, sine], axis=0).T

    load_keys.wait()
    load_gain.wait()
    gains = gains_row[...]

    def turn_sequence(s, _):
        def turn_rows(c, largest):
            rows = pl.ds(pl.multiple_of(c * CHUNK, CHUNK), CHUNK)
            wide = raw[s, rows, :].astype(jnp.float32)
            mean = jnp.mean(wide * wide, axis=-1, keepdims=True)
            wide = wide * lax.rsqrt(mean + 1e-06) * gains
            out = wide * cosines[rows, :] + pltpu.roll(wide, HALF, 1) * sines[rows, :]
            turned[s, rows, :] = out
            return jnp.maximum(largest, jnp.max(jnp.abs(out).reshape(CHUNK // 8, 8, LANES), axis=0))

        largest = lax.fori_loop(0, ROWS // CHUNK, turn_rows, jnp.zeros((8, LANES), jnp.float32))
        maxes[0, pl.ds(s, 1), :] = jnp.max(largest, axis=0, keepdims=True)
        return 0

    lax.fori_loop(0, SEQS, turn_sequence, 0)

    shared = [
        pltpu.make_async_remote_copy(
            src_ref=maxes.at[0],
            dst_ref=maxes.at[1 + i],
            send_sem=m_send.at[i],
            recv_sem=m_recv.at[i],
            device_id=ids[i],
            device_id_type=MESH,
        )
        for i in range(PEERS)
    ]
    for copy in shared:
        copy.start()
    copies += send_values(1, FIRST_ROWS, ROWS - FIRST_ROWS)
    for copy in shared:
        copy.wait()

    largest = maxes[0]
    for i in range(PEERS):
        largest = jnp.maximum(largest, maxes[1 + i])
    maxes[0] = largest
    scale[...] = maxes[0, pl.ds(me, 1), :]

    def scale_sequence(s, _):
        inverse = 1.0 / maxes[0, pl.ds(s, 1), :]

        def scale_rows(c, _):
            rows = pl.ds(pl.multiple_of(c * CHUNK, CHUNK), CHUNK)
            narrow[s, rows, :] = (turned[s, rows, :] * inverse).astype(jnp.bfloat16)
            return 0

        lax.fori_loop(0, ROWS // CHUNK, scale_rows, 0)
        return 0

    lax.fori_loop(0, SEQS, scale_sequence, 0)

    sent = [
        pltpu.make_async_remote_copy(
            src_ref=narrow.at[index[i]],
            dst_ref=kland.at[pl.ds(pl.multiple_of(me * ROWS, ROWS), ROWS)],
            send_sem=k_send.at[i],
            recv_sem=k_recv.at[i],
            device_id=ids[i],
            device_id_type=MESH,
        )
        for i in range(PEERS)
    ]
    for copy in sent:
        copy.start()

    def keep_rows(c, _):
        rows = pl.ds(pl.multiple_of(me * ROWS + c * CHUNK, CHUNK), CHUNK)
        kland[rows, :] = narrow[me, pl.ds(pl.multiple_of(c * CHUNK, CHUNK), CHUNK), :]
        return 0

    lax.fori_loop(0, ROWS // CHUNK, keep_rows, 0)
    keep.wait()
    for copy in copies + sent:
        copy.wait()


PIECES = 8


def store(kland, vland, scale, kout, vout, scale_out, sems):
    rows = TOTAL // PIECES
    copies = []
    for i, (source, target) in enumerate(((kland, kout), (vland, vout))):
        for j in range(PIECES):
            part = pl.ds(j * rows, rows)
            copies.append(pltpu.make_async_copy(source.at[part], target.at[part], sems.at[i, j]))
    copies.append(pltpu.make_async_copy(scale, scale_out, sems.at[2, 0]))
    for copy in copies:
        copy.start()
    for copy in copies:
        copy.wait()


def local(raw_keys, raw_values, turn_angle, key_gain):
    shape = (SEQS, ROWS, LANES)
    hbm = pl.BlockSpec(memory_space=pltpu.HBM)
    vmem = pl.BlockSpec(memory_space=pltpu.VMEM)
    kland, vland, scale = pl.pallas_call(
        exchange,
        name="exchange",
        out_shape=(
            pltpu.VMEM((TOTAL, LANES), jnp.bfloat16),
            pltpu.VMEM((TOTAL, LANES), jnp.bfloat16),
            pltpu.VMEM((1, LANES), jnp.float32),
        ),
        in_specs=[hbm, hbm, hbm, hbm],
        out_specs=(vmem, vmem, vmem),
        scratch_shapes=[
            pltpu.VMEM(shape, jnp.bfloat16),
            pltpu.VMEM(shape, jnp.float32),
            pltpu.VMEM(shape, jnp.bfloat16),
            pltpu.VMEM((HALF, ROWS), jnp.float32),
            pltpu.VMEM((1, LANES), jnp.float32),
            pltpu.VMEM((ROWS, LANES), jnp.float32),
            pltpu.VMEM((ROWS, LANES), jnp.float32),
            pltpu.VMEM((1 + PEERS, SEQS, LANES), jnp.float32),
            pltpu.SemaphoreType.DMA((4,)),
            pltpu.SemaphoreType.DMA((2, PEERS)),
            pltpu.SemaphoreType.DMA((2, PEERS)),
            pltpu.SemaphoreType.DMA((PEERS,)),
            pltpu.SemaphoreType.DMA((PEERS,)),
            pltpu.SemaphoreType.DMA((PEERS,)),
            pltpu.SemaphoreType.DMA((PEERS,)),
        ],
        compiler_params=pltpu.CompilerParams(
            collective_id=0, has_side_effects=True, vmem_limit_bytes=40 * 2**20
        ),
    )(
        *(
            pltpu.with_memory_space_constraint(array, pltpu.HBM)
            for array in (
                raw_keys.reshape(shape),
                raw_values.reshape(shape),
                turn_angle.T,
                key_gain.reshape(1, LANES),
            )
        )
    )
    kout, vout, scale = pl.pallas_call(
        store,
        name="store",
        out_shape=(
            jax.ShapeDtypeStruct((TOTAL, LANES), jnp.bfloat16),
            jax.ShapeDtypeStruct((TOTAL, LANES), jnp.bfloat16),
            jax.ShapeDtypeStruct((1, LANES), jnp.float32),
        ),
        in_specs=[vmem, vmem, vmem],
        out_specs=(hbm, hbm, hbm),
        scratch_shapes=[pltpu.SemaphoreType.DMA((3, PIECES))],
        compiler_params=pltpu.CompilerParams(vmem_limit_bytes=2**20),
    )(kland, vland, scale)
    whole = (1, TOTAL, 1, LANES)
    return kout.reshape(whole), vout.reshape(whole), scale.reshape(1, 1, LANES)


def solution(mesh):
    in_specs = (
        P(None, ("farcp", "nearcp"), "model", None),
        P(None, ("farcp", "nearcp"), "model", None),
        P(),
        P(),
    )
    out_specs = (
        P(("farcp", "nearcp"), None, "model", None),
        P(("farcp", "nearcp"), None, "model", None),
        P(("farcp", "nearcp"), "model", None),
    )
    return jax.shard_map(local, mesh=mesh, in_specs=in_specs, out_specs=out_specs, check_vma=False)
```

time: 132 us -> 110 us (0.83); the launches traced: 130 us -> 110 us
  Pallas kernels: 0 us -> 109 us
  local copies, waits for them, and re-layouts: 45 us -> 0 us
  other arithmetic: 43 us -> 0 us
  waiting for transfers between devices: 23.2 us -> 0 us
  starting transfers between devices: 18 us -> 0 us
    pallas_call x0 -> x2, Pallas kernels: none -> 109 us  [the longest x1 106 us: local(): pl.pallas_call(exchange, name='exchange', out_shape=(pltpu.VMEM((TOTAL, L...]
    cos x1 -> x0, local copies, waits for them, and re-layouts: 31.5 us -> none  [apply_rotary(): jnp.cos(angle)[None, :, None, :]]
    all_to_all x2 -> x0, waiting for transfers between devices: 23.2 us -> none  [the longest x1 15.4 us: local(): lax.all_to_all(raw_keys, ('farcp', 'nearcp'), split_axis=0, concat_axis=1...]
    all_to_all x2 -> x0, starting transfers between devices: 18 us -> none  [the longest x1 9.13 us: local(): lax.all_to_all(raw_keys, ('farcp', 'nearcp'), split_axis=0, concat_axis=1...]
    sub x1 -> x0, other arithmetic: 17.3 us -> none  [apply_rotary(): first * cosine - second * sine]
    unnamed x11 -> x0, local copies, waits for them, and re-layouts: 13.5 us -> none
    mul x1 -> x0, other arithmetic: 9.9 us -> none  [scale_rows(): vectors * lax.rsqrt(jnp.mean(vectors * vectors, axis=-1, keepdims=True) +...]
    reduce_max x1 -> x0, other arithmetic: 7.69 us -> none  [local(): key_scale = jnp.max(jnp.abs(turned_keys), axis=1)]
  transfers between devices with their start and end apart: 2 -> 0, of which waited for: 2 -> 0; matrix products, arithmetic and copies ran while one was open for 63% -> 0% of each run, Pallas kernels for 0% -> 0%
where the time goes in v1:
time: 110 us
  Pallas kernels  109 us (99%)
    pallas_call x1, Pallas kernels, local(): pl.pallas_call(exchange, name='exchange', out_shape=(pltpu.VMEM((TOTAL, L...  106 us
    pallas_call x1, Pallas kernels, local(): pl.pallas_call(store, name='store', out_shape=(jax.ShapeDtypeStruct((TOTA...  3.49 us

profile of v1, /device:TPU:1, one launch (start us, length us, event | category | flops | bytes accessed | tf_op | source)
XLA Modules:
  0.0 109.7 jit_solution(228601488600130383)
XLA Ops:
  0.6 105.6 %exchange.1 = (bf16[16384,128]{1,0:T(8,128)(2,1)S(1)}, bf16[16384,128]{1,0:T(8,128)(2,1)S(1)}, f32[1,128]{1,0:T(1,128)S(1)}) custom-call(bf16[16,1024,128]{2,1,0:T(8,128)(2,1)} %bitcast.7, bf16[16,1024,128]{2,1,0:T(8,128)(2,1)} %bitcast.8, f32[64,16384]{1,0:T(8,128)} %bitcast.9, f32[1,128]{1,0:T(1,128)} %bitcast.10), custom_call_target="tpu_custom_call" | custom-call | tf_op jit(solution)/shard_map/exchange/pallas_call | solution.py:193
  106.2 3.5 %store.1 = (bf16[16384,128]{1,0:T(8,128)(2,1)}, bf16[16384,128]{1,0:T(8,128)(2,1)}, f32[1,128]{1,0:T(1,128)}) custom-call(bf16[16384,128]{1,0:T(8,128)(2,1)S(1)} %get-tuple-element.9.kland, bf16[16384,128]{1,0:T(8,128)(2,1)S(1)} %get-tuple-element.10.vland, f32[1,128]{1,0:T(1,128)S(1)} %get-tuple-element.11.scale), custom_call_target="tpu_custom_call" | custom-call | tf_op jit(solution)/shard_map/store/pallas_call | solution.py:234

commit v2 on v1

v2 whole, which is shorter than its diff:
```python
import jax
import jax.numpy as jnp
from jax import lax
from jax.experimental import pallas as pl
from jax.experimental.pallas import tpu as pltpu
from jax.sharding import PartitionSpec as P

MESH = pl.DeviceIdType.MESH
SEQS, ROWS, LANES, HALF = 16, 1024, 128, 64
TOTAL = SEQS * ROWS
CHUNK = 128
FIRST_ROWS = 768
Z_FIRST = 3
V_ONE, V_TWO = 2, 4


STEPS = [(dx, c) for c in (0, 1) for dx in (1, 3, 2)]
RELAYED = len(STEPS)
PLANE = RELAYED + 1
COPIES = 64


def exchange(
    keys, values, angle, gain,
    kland, vland, scale,
    raw, turned, narrow, krelay, vrelay, angles, gains_row, cosines, sines, maxes,
    local_sem, send_sem, recv_sem,
):
    far, near, model = lax.axis_index("farcp"), lax.axis_index("nearcp"), lax.axis_index("model")
    core, x, z = near % 2, ((near // 2) % 2) * 2 + far, near // 4
    used = [0]

    def place(dx, dz, dc):
        px, pz, pc = (x + dx) % 4, (z + dz) % 2, (core + dc) % 2
        return px % 2, pz * 4 + (px // 2) * 2 + pc

    def device(dx, dz, dc):
        return (*place(dx, dz, dc), model)

    def index(dx, dz, dc):
        f, n = place(dx, dz, dc)
        return f * 8 + n

    def block(owner, first=0, rows=ROWS):
        return pl.ds(pl.multiple_of(owner * ROWS + first, CHUNK), rows)

    me, across = far * 8 + near, index(0, 1, 0)

    def send(source, target, *step):
        i = used[0]
        used[0] += 1
        copy = pltpu.make_async_remote_copy(
            src_ref=source,
            dst_ref=target,
            send_sem=send_sem.at[i],
            recv_sem=recv_sem.at[i],
            device_id=device(*step),
            device_id_type=MESH,
        )
        copy.start()
        return copy

    load_keys = pltpu.make_async_copy(keys, raw, local_sem.at[0])
    load_angles = pltpu.make_async_copy(angle.at[:, block(me)], angles, local_sem.at[1])
    load_gain = pltpu.make_async_copy(gain, gains_row, local_sem.at[2])
    keep = pltpu.make_async_copy(values.at[me], vland.at[block(me)], local_sem.at[3])

    barrier = pltpu.get_barrier_semaphore()
    greeted = [(0, 1, 0), (0, 1, 1), (0, 0, 1)] + [(dx, 0, dc) for dx, dc in STEPS]
    for step in greeted:
        pl.semaphore_signal(barrier, inc=1, device_id=device(*step), device_id_type=MESH)
    load_angles.start()
    load_gain.start()
    load_keys.start()
    pl.semaphore_wait(barrier, len(greeted))

    def relay_out(source, relay, i):
        dx, dc = STEPS[i]
        return send(source.at[index(dx, 1, dc)], relay.at[i], 0, 1, 0)

    def forward(relay, land, i):
        dx, dc = STEPS[i]
        return send(relay.at[i], land.at[block(across)], dx, 0, dc)

    def along_x(source, land, i, first, rows):
        dx, dc = STEPS[i]
        part = pl.ds(first, rows)
        return send(source.at[index(dx, 0, dc), part], land.at[block(me, first, rows)], dx, 0, dc)

    def along_z(source, land, dc):
        return send(source.at[index(0, 1, dc)], land.at[block(me)], 0, 1, dc)

    def to_sibling(source, land):
        return send(source.at[index(0, 0, 1)], land.at[block(me)], 0, 0, 1)

    vz, copies = [], []
    for i in range(RELAYED):
        if i < Z_FIRST:
            vz.append(relay_out(values, vrelay, i))
        copies.append(along_x(values, vland, i, 0, FIRST_ROWS))
    copies.append(to_sibling(values, vland))
    keep.start()

    load_angles.wait()
    for c in range(ROWS // CHUNK):
        a = angles[:, c * CHUNK : (c + 1) * CHUNK]
        cosine, sine = jnp.cos(a), jnp.sin(a)
        rows = pl.ds(c * CHUNK, CHUNK)
        cosines[rows, :] = jnp.concatenate([cosine, cosine], axis=0).T
        sines[rows, :] = jnp.concatenate([-sine, sine], axis=0).T

    load_gain.wait()
    load_keys.wait()
    gains = gains_row[...]

    def turn_sequence(s, _):
        largest = jnp.zeros((8, LANES), jnp.float32)
        for c in range(ROWS // CHUNK):
            rows = pl.ds(c * CHUNK, CHUNK)
            wide = raw[s, rows, :].astype(jnp.float32)
            mean = jnp.mean(wide * wide, axis=-1, keepdims=True)
            wide = wide * lax.rsqrt(mean + 1e-06) * gains
            out = wide * cosines[rows, :] + pltpu.roll(wide, HALF, 1) * sines[rows, :]
            turned[s, rows, :] = out
            largest = jnp.maximum(
                largest, jnp.max(jnp.abs(out).reshape(CHUNK // 8, 8, LANES), axis=0)
            )
        maxes[0, pl.ds(s, 1), :] = jnp.max(largest, axis=0, keepdims=True)
        return 0

    lax.fori_loop(0, SEQS, turn_sequence, 0)

    first = send(maxes.at[0], maxes.at[1], 0, 1, 0)
    for i in range(Z_FIRST, RELAYED):
        vz.append(relay_out(values, vrelay, i))
    for dc in (0, 1):
        copies.append(along_z(values, vland, dc))
    if FIRST_ROWS < ROWS:
        for i in range(RELAYED):
            copies.append(along_x(values, vland, i, FIRST_ROWS, ROWS - FIRST_ROWS))
    for i in range(V_ONE):
        vz[i].wait_recv()
        copies.append(forward(vrelay, vland, i))
    first.wait()
    maxes[2] = jnp.maximum(maxes[0], maxes[1])
    second = [
        send(maxes.at[2], maxes.at[3 + i], dx, 0, dc) for i, (dx, dc) in enumerate(STEPS + [(0, 1)])
    ]
    for i in range(V_ONE, V_TWO):
        vz[i].wait_recv()
        copies.append(forward(vrelay, vland, i))
    for copy in second:
        copy.wait()
    largest = maxes[2]
    for i in range(PLANE):
        largest = jnp.maximum(largest, maxes[3 + i])
    maxes[0] = largest
    scale[...] = maxes[0, pl.ds(me, 1), :]

    def scale_sequence(s, _):
        inverse = 1.0 / maxes[0, pl.ds(s, 1), :]
        for c in range(ROWS // CHUNK):
            rows = pl.ds(c * CHUNK, CHUNK)
            narrow[s, rows, :] = (turned[s, rows, :] * inverse).astype(jnp.bfloat16)
        return 0

    lax.fori_loop(0, SEQS, scale_sequence, 0)

    kz = [relay_out(narrow, krelay, i) for i in range(RELAYED)]
    for dc in (0, 1):
        copies.append(along_z(narrow, kland, dc))
    for i in range(V_TWO, RELAYED):
        vz[i].wait_recv()
        copies.append(forward(vrelay, vland, i))
    for i in range(RELAYED):
        copies.append(along_x(narrow, kland, i, 0, ROWS))
    copies.append(to_sibling(narrow, kland))

    def keep_rows(c, _):
        kland[block(me, c * CHUNK, CHUNK), :] = narrow[
            me, pl.ds(pl.multiple_of(c * CHUNK, CHUNK), CHUNK), :
        ]
        return 0

    lax.fori_loop(0, ROWS // CHUNK, keep_rows, 0)
    for i in range(RELAYED):
        kz[i].wait_recv()
        copies.append(forward(krelay, kland, i))
    keep.wait()
    for copy in vz + kz:
        copy.wait_send()
    for copy in copies:
        copy.wait()


PIECES = 8


def store(kland, vland, scale, kout, vout, scale_out, sems):
    rows = TOTAL // PIECES
    copies = []
    for i, (source, target) in enumerate(((kland, kout), (vland, vout))):
        for j in range(PIECES):
            part = pl.ds(j * rows, rows)
            copies.append(pltpu.make_async_copy(source.at[part], target.at[part], sems.at[i, j]))
    copies.append(pltpu.make_async_copy(scale, scale_out, sems.at[2, 0]))
    for copy in copies:
        copy.start()
    for copy in copies:
        copy.wait()


def local(raw_keys, raw_values, turn_angle, key_gain):
    shape = (SEQS, ROWS, LANES)
    hbm = pl.BlockSpec(memory_space=pltpu.HBM)
    vmem = pl.BlockSpec(memory_space=pltpu.VMEM)
    kland, vland, scale = pl.pallas_call(
        exchange,
        name="exchange",
        out_shape=(
            pltpu.VMEM((TOTAL, LANES), jnp.bfloat16),
            pltpu.VMEM((TOTAL, LANES), jnp.bfloat16),
            pltpu.VMEM((1, LANES), jnp.float32),
        ),
        in_specs=[hbm, hbm, hbm, hbm],
        out_specs=(vmem, vmem, vmem),
        scratch_shapes=[
            pltpu.VMEM(shape, jnp.bfloat16),
            pltpu.VMEM(shape, jnp.float32),
            pltpu.VMEM(shape, jnp.bfloat16),
            pltpu.VMEM((RELAYED, ROWS, LANES), jnp.bfloat16),
            pltpu.VMEM((RELAYED, ROWS, LANES), jnp.bfloat16),
            pltpu.VMEM((HALF, ROWS), jnp.float32),
            pltpu.VMEM((1, LANES), jnp.float32),
            pltpu.VMEM((ROWS, LANES), jnp.float32),
            pltpu.VMEM((ROWS, LANES), jnp.float32),
            pltpu.VMEM((3 + PLANE, SEQS, LANES), jnp.float32),
            pltpu.SemaphoreType.DMA((4,)),
            pltpu.SemaphoreType.DMA((COPIES,)),
            pltpu.SemaphoreType.DMA((COPIES,)),
        ],
        compiler_params=pltpu.CompilerParams(
            collective_id=0, has_side_effects=True, vmem_limit_bytes=40 * 2**20
        ),
    )(
        *(
            pltpu.with_memory_space_constraint(array, pltpu.HBM)
            for array in (
                raw_keys.reshape(shape),
                raw_values.reshape(shape),
                turn_angle.T,
                key_gain.reshape(1, LANES),
            )
        )
    )
    kout, vout, scale = pl.pallas_call(
        store,
        name="store",
        out_shape=(
            jax.ShapeDtypeStruct((TOTAL, LANES), jnp.bfloat16),
            jax.ShapeDtypeStruct((TOTAL, LANES), jnp.bfloat16),
            jax.ShapeDtypeStruct((1, LANES), jnp.float32),
        ),
        in_specs=[vmem, vmem, vmem],
        out_specs=(hbm, hbm, hbm),
        scratch_shapes=[pltpu.SemaphoreType.DMA((3, PIECES))],
        compiler_params=pltpu.CompilerParams(vmem_limit_bytes=2**20),
    )(kland, vland, scale)
    whole = (1, TOTAL, 1, LANES)
    return kout.reshape(whole), vout.reshape(whole), scale.reshape(1, 1, LANES)


def solution(mesh):
    in_specs = (
        P(None, ("farcp", "nearcp"), "model", None),
        P(None, ("farcp", "nearcp"), "model", None),
        P(),
        P(),
    )
    out_specs = (
        P(("farcp", "nearcp"), None, "model", None),
        P(("farcp", "nearcp"), None, "model", None),
        P(("farcp", "nearcp"), "model", None),
    )
    return jax.shard_map(local, mesh=mesh, in_specs=in_specs, out_specs=out_specs, check_vma=False)
```

time: 110 us -> 105 us (0.955)
  Pallas kernels: 109 us -> 105 us
    pallas_call x1, Pallas kernels: 106 us -> 101 us  [local(): pl.pallas_call(exchange, name='exchange', out_shape=(pltpu.VMEM((TOTAL, L...]
where the time goes in v2:
time: 105 us
  Pallas kernels  105 us (100%)
    pallas_call x1, Pallas kernels, local(): pl.pallas_call(exchange, name='exchange', out_shape=(pltpu.VMEM((TOTAL, L...  101 us
    pallas_call x1, Pallas kernels, local(): pl.pallas_call(store, name='store', out_shape=(jax.ShapeDtypeStruct((TOTA...  3.49 us

profile of v2, /device:TPU:1, one launch (start us, length us, event | category | flops | bytes accessed | tf_op | source)
XLA Modules:
  0.0 105.2 jit_solution(8963543711316688097)
XLA Ops:
  0.6 101.0 %exchange.1 = (bf16[16384,128]{1,0:T(8,128)(2,1)S(1)}, bf16[16384,128]{1,0:T(8,128)(2,1)S(1)}, f32[1,128]{1,0:T(1,128)S(1)}) custom-call(bf16[16,1024,128]{2,1,0:T(8,128)(2,1)} %bitcast.7, bf16[16,1024,128]{2,1,0:T(8,128)(2,1)} %bitcast.8, f32[64,16384]{1,0:T(8,128)} %bitcast.9, f32[1,128]{1,0:T(1,128)} %bitcast.10), custom_call_target="tpu_custom_call" | custom-call | tf_op jit(solution)/shard_map/exchange/pallas_call | solution.py:217
  101.7 3.5 %store.1 = (bf16[16384,128]{1,0:T(8,128)(2,1)}, bf16[16384,128]{1,0:T(8,128)(2,1)}, f32[1,128]{1,0:T(1,128)}) custom-call(bf16[16384,128]{1,0:T(8,128)(2,1)S(1)} %get-tuple-element.9.kland, bf16[16384,128]{1,0:T(8,128)(2,1)S(1)} %get-tuple-element.10.vland, f32[1,128]{1,0:T(1,128)S(1)} %get-tuple-element.11.scale), custom_call_target="tpu_custom_call" | custom-call | tf_op jit(solution)/shard_map/store/pallas_call | solution.py:256

commit v3 on v2

--- a/solution.py
+++ b/solution.py
@@ -24,7 +24,7 @@
     keys, values, angle, gain,
     kland, vland, scale,
     raw, turned, narrow, krelay, vrelay, angles, gains_row, cosines, sines, maxes,
-    local_sem, send_sem, recv_sem,
+    local_sem, ready_sem, send_sem, recv_sem,
 ):
     far, near, model = lax.axis_index("farcp"), lax.axis_index("nearcp"), lax.axis_index("model")
     core, x, z = near % 2, ((near // 2) % 2) * 2 + far, near // 4
@@ -46,10 +46,10 @@
 
     me, across = far * 8 + near, index(0, 1, 0)
 
-    def send(source, target, *step):
+    def plan(source, target, *step):
         i = used[0]
         used[0] += 1
-        copy = pltpu.make_async_remote_copy(
+        return pltpu.make_async_remote_copy(
             src_ref=source,
             dst_ref=target,
             send_sem=send_sem.at[i],
@@ -57,6 +57,13 @@
             device_id=device(*step),
             device_id_type=MESH,
         )
+
+    def start(copies):
+        for copy in copies:
+            copy.start()
+
+    def send(*way):
+        copy = plan(*way)
         copy.start()
         return copy
 
@@ -66,17 +73,18 @@
     keep = pltpu.make_async_copy(values.at[me], vland.at[block(me)], local_sem.at[3])
 
     barrier = pltpu.get_barrier_semaphore()
-    greeted = [(0, 1, 0), (0, 1, 1), (0, 0, 1)] + [(dx, 0, dc) for dx, dc in STEPS]
-    for step in greeted:
-        pl.semaphore_signal(barrier, inc=1, device_id=device(*step), device_id_type=MESH)
+    greeted = [device(0, 1, core), device(0, 0, 1)] + [device(dx, 0, 1 - core) for dx in (1, 3, 2)]
+    for target in greeted:
+        pl.semaphore_signal(barrier, inc=1, device_id=target, device_id_type=MESH)
     load_angles.start()
     load_gain.start()
     load_keys.start()
-    pl.semaphore_wait(barrier, len(greeted))
+    pl.semaphore_wait(barrier, 3 + 4 * core)
+    pl.semaphore_signal(ready_sem, inc=1, device_id=device(0, 0, 1), device_id_type=MESH)
 
     def relay_out(source, relay, i):
         dx, dc = STEPS[i]
-        return send(source.at[index(dx, 1, dc)], relay.at[i], 0, 1, 0)
+        return plan(source.at[index(dx, 1, dc)], relay.at[i], 0, 1, 0)
 
     def forward(relay, land, i):
         dx, dc = STEPS[i]
@@ -85,7 +93,7 @@
     def along_x(source, land, i, first, rows):
         dx, dc = STEPS[i]
         part = pl.ds(first, rows)
-        return send(source.at[index(dx, 0, dc), part], land.at[block(me, first, rows)], dx, 0, dc)
+        return plan(source.at[index(dx, 0, dc), part], land.at[block(me, first, rows)], dx, 0, dc)
 
     def along_z(source, land, dc):
         return send(source.at[index(0, 1, dc)], land.at[block(me)], 0, 1, dc)
@@ -93,12 +101,28 @@
     def to_sibling(source, land):
         return send(source.at[index(0, 0, 1)], land.at[block(me)], 0, 0, 1)
 
-    vz, copies = [], []
-    for i in range(RELAYED):
-        if i < Z_FIRST:
-            vz.append(relay_out(values, vrelay, i))
-        copies.append(along_x(values, vland, i, 0, FIRST_ROWS))
-    copies.append(to_sibling(values, vland))
+    vz = [relay_out(values, vrelay, i) for i in range(RELAYED)]
+    vx = [along_x(values, vland, i, 0, FIRST_ROWS) for i in range(RELAYED)]
+
+    @pl.when(core == 0)
+    def _():
+        start(vz[:Z_FIRST])
+
+    @pl.when(core == 1)
+    def _():
+        start(vx)
+
+    pl.semaphore_wait(ready_sem, 1)
+
+    @pl.when(core == 0)
+    def _():
+        start(vx)
+
+    @pl.when(core == 1)
+    def _():
+        start(vz[:Z_FIRST])
+
+    copies = vx + [to_sibling(values, vland)]
     keep.start()
 
     load_angles.wait()
@@ -131,13 +155,13 @@
     lax.fori_loop(0, SEQS, turn_sequence, 0)
 
     first = send(maxes.at[0], maxes.at[1], 0, 1, 0)
-    for i in range(Z_FIRST, RELAYED):
-        vz.append(relay_out(values, vrelay, i))
+    start(vz[Z_FIRST:])
     for dc in (0, 1):
         copies.append(along_z(values, vland, dc))
     if FIRST_ROWS < ROWS:
-        for i in range(RELAYED):
-            copies.append(along_x(values, vland, i, FIRST_ROWS, ROWS - FIRST_ROWS))
+        rest = [along_x(values, vland, i, FIRST_ROWS, ROWS - FIRST_ROWS) for i in range(RELAYED)]
+        start(rest)
+        copies += rest
     for i in range(V_ONE):
         vz[i].wait_recv()
         copies.append(forward(vrelay, vland, i))
@@ -167,13 +191,15 @@
     lax.fori_loop(0, SEQS, scale_sequence, 0)
 
     kz = [relay_out(narrow, krelay, i) for i in range(RELAYED)]
+    start(kz)
     for dc in (0, 1):
         copies.append(along_z(narrow, kland, dc))
     for i in range(V_TWO, RELAYED):
         vz[i].wait_recv()
         copies.append(forward(vrelay, vland, i))
-    for i in range(RELAYED):
-        copies.append(along_x(narrow, kland, i, 0, ROWS))
+    kx = [along_x(narrow, kland, i, 0, ROWS) for i in range(RELAYED)]
+    start(kx)
+    copies += kx
     copies.append(to_sibling(narrow, kland))
 
     def keep_rows(c, _):
@@ -193,7 +219,7 @@
         copy.wait()
 
 
-PIECES = 8
+PIECES = 2
 
 
 def store(kland, vland, scale, kout, vout, scale_out, sems):
@@ -236,6 +262,7 @@
             pltpu.VMEM((ROWS, LANES), jnp.float32),
             pltpu.VMEM((3 + PLANE, SEQS, LANES), jnp.float32),
             pltpu.SemaphoreType.DMA((4,)),
+            pltpu.SemaphoreType.REGULAR,
             pltpu.SemaphoreType.DMA((COPIES,)),
             pltpu.SemaphoreType.DMA((COPIES,)),
         ],

time: 105 us -> 103 us (0.981)
  Pallas kernels: 105 us -> 102 us
    pallas_call x1, Pallas kernels: 101 us -> 98.8 us  [local(): pl.pallas_call(exchange, name='exchange', out_shape=(pltpu.VMEM((TOTAL, L...]
where the time goes in v3:
time: 103 us
  Pallas kernels  102 us (99%)
    pallas_call x1, Pallas kernels, local(): pl.pallas_call(exchange, name='exchange', out_shape=(pltpu.VMEM((TOTAL, L...  98.8 us
    pallas_call x1, Pallas kernels, local(): pl.pallas_call(store, name='store', out_shape=(jax.ShapeDtypeStruct((TOTA...  3.39 us

profile of v3, /device:TPU:1, one launch (start us, length us, event | category | flops | bytes accessed | tf_op | source)
XLA Modules:
  0.0 102.9 jit_solution(936481390663822820)
XLA Ops:
  0.6 98.8 %exchange.1 = (bf16[16384,128]{1,0:T(8,128)(2,1)S(1)}, bf16[16384,128]{1,0:T(8,128)(2,1)S(1)}, f32[1,128]{1,0:T(1,128)S(1)}) custom-call(bf16[16,1024,128]{2,1,0:T(8,128)(2,1)} %bitcast.7, bf16[16,1024,128]{2,1,0:T(8,128)(2,1)} %bitcast.8, f32[64,16384]{1,0:T(8,128)} %bitcast.9, f32[1,128]{1,0:T(1,128)} %bitcast.10), custom_call_target="tpu_custom_call" | custom-call | tf_op jit(solution)/shard_map/exchange/pallas_call | solution.py:243
  99.5 3.4 %store.1 = (bf16[16384,128]{1,0:T(8,128)(2,1)}, bf16[16384,128]{1,0:T(8,128)(2,1)}, f32[1,128]{1,0:T(1,128)}) custom-call(bf16[16384,128]{1,0:T(8,128)(2,1)S(1)} %get-tuple-element.9.kland, bf16[16384,128]{1,0:T(8,128)(2,1)S(1)} %get-tuple-element.10.vland, f32[1,128]{1,0:T(1,128)S(1)} %get-tuple-element.11.scale), custom_call_target="tpu_custom_call" | custom-call | tf_op jit(solution)/shard_map/store/pallas_call | solution.py:283

commit v4 on v3

--- a/solution.py
+++ b/solution.py
@@ -14,8 +14,8 @@
 V_ONE, V_TWO = 2, 4
 
 
-STEPS = [(dx, c) for c in (0, 1) for dx in (1, 3, 2)]
-RELAYED = len(STEPS)
+ALONG_X = (1, 3, 2)
+RELAYED = 2 * len(ALONG_X)
 PLANE = RELAYED + 1
 COPIES = 64
 
@@ -46,26 +46,26 @@
 
     me, across = far * 8 + near, index(0, 1, 0)
 
-    def plan(source, target, *step):
-        i = used[0]
-        used[0] += 1
+    steps = [(dx, (core + to) % 2, n) for to in (1, 0) for n, dx in enumerate(ALONG_X)]
+    steps = [(dx, dc, n + len(ALONG_X) * dc) for dx, dc, n in steps]
+
+    def plan(source, target, dx, dz, dc, slot):
         return pltpu.make_async_remote_copy(
             src_ref=source,
             dst_ref=target,
-            send_sem=send_sem.at[i],
-            recv_sem=recv_sem.at[i],
-            device_id=device(*step),
+            send_sem=send_sem.at[slot],
+            recv_sem=recv_sem.at[slot],
+            device_id=device(dx, dz, dc),
             device_id_type=MESH,
         )
+
+    def slots(count):
+        used[0] += count
+        return used[0] - count
 
     def start(copies):
         for copy in copies:
             copy.start()
-
-    def send(*way):
-        copy = plan(*way)
-        copy.start()
-        return copy
 
     load_keys = pltpu.make_async_copy(keys, raw, local_sem.at[0])
     load_angles = pltpu.make_async_copy(angle.at[:, block(me)], angles, local_sem.at[1])
@@ -82,27 +82,42 @@
     pl.semaphore_wait(barrier, 3 + 4 * core)
     pl.semaphore_signal(ready_sem, inc=1, device_id=device(0, 0, 1), device_id_type=MESH)
 
-    def relay_out(source, relay, i):
-        dx, dc = STEPS[i]
-        return plan(source.at[index(dx, 1, dc)], relay.at[i], 0, 1, 0)
-
-    def forward(relay, land, i):
-        dx, dc = STEPS[i]
-        return send(relay.at[i], land.at[block(across)], dx, 0, dc)
-
-    def along_x(source, land, i, first, rows):
-        dx, dc = STEPS[i]
-        part = pl.ds(first, rows)
-        return plan(source.at[index(dx, 0, dc), part], land.at[block(me, first, rows)], dx, 0, dc)
-
-    def along_z(source, land, dc):
-        return send(source.at[index(0, 1, dc)], land.at[block(me)], 0, 1, dc)
+    def relay_out(source, relay):
+        base = slots(RELAYED)
+        return [
+            plan(source.at[index(dx, 1, dc)], relay.at[i], 0, 1, 0, base + i) for dx, dc, i in steps
+        ]
+
+    def forward(relay, land):
+        base = slots(RELAYED)
+        return [
+            plan(relay.at[i], land.at[block(across)], dx, 0, dc, base + i) for dx, dc, i in steps
+        ]
+
+    def along_x(source, land, first, rows):
+        base, part = slots(RELAYED), pl.ds(first, rows)
+        return [
+            plan(
+                source.at[index(dx, 0, dc), part],
+                land.at[block(me, first, rows)],
+                dx, 0, dc, base + i,
+            )
+            for dx, dc, i in steps
+        ]
+
+    def along_z(source, land):
+        base = slots(2)
+        return [
+            plan(source.at[index(0, 1, dc)], land.at[block(me)], 0, 1, dc, base + dc)
+            for dc in ((core + 1) % 2, core)
+        ]
 
     def to_sibling(source, land):
-        return send(source.at[index(0, 0, 1)], land.at[block(me)], 0, 0, 1)
-
-    vz = [relay_out(values, vrelay, i) for i in range(RELAYED)]
-    vx = [along_x(values, vland, i, 0, FIRST_ROWS) for i in range(RELAYED)]
+        return [plan(source.at[index(0, 0, 1)], land.at[block(me)], 0, 0, 1, slots(1))]
+
+    vz, vf = relay_out(values, vrelay), forward(vrelay, vland)
+    vx = along_x(values, vland, 0, FIRST_ROWS)
+    side = to_sibling(values, vland)
 
     @pl.when(core == 0)
     def _():
@@ -122,7 +137,8 @@
     def _():
         start(vz[:Z_FIRST])
 
-    copies = vx + [to_sibling(values, vland)]
+    start(side)
+    copies = vx + vf + side
     keep.start()
 
     load_angles.wait()
@@ -154,25 +170,27 @@
 
     lax.fori_loop(0, SEQS, turn_sequence, 0)
 
-    first = send(maxes.at[0], maxes.at[1], 0, 1, 0)
+    first = plan(maxes.at[0], maxes.at[1], 0, 1, 0, slots(1))
+    first.start()
     start(vz[Z_FIRST:])
-    for dc in (0, 1):
-        copies.append(along_z(values, vland, dc))
-    if FIRST_ROWS < ROWS:
-        rest = [along_x(values, vland, i, FIRST_ROWS, ROWS - FIRST_ROWS) for i in range(RELAYED)]
-        start(rest)
-        copies += rest
+    straight = along_z(values, vland)
+    rest = along_x(values, vland, FIRST_ROWS, ROWS - FIRST_ROWS)
+    start(straight + rest)
+    copies += straight + rest
     for i in range(V_ONE):
         vz[i].wait_recv()
-        copies.append(forward(vrelay, vland, i))
+        vf[i].start()
     first.wait()
     maxes[2] = jnp.maximum(maxes[0], maxes[1])
+    base = slots(PLANE)
     second = [
-        send(maxes.at[2], maxes.at[3 + i], dx, 0, dc) for i, (dx, dc) in enumerate(STEPS + [(0, 1)])
+        plan(maxes.at[2], maxes.at[3 + i], dx, 0, dc, base + i)
+        for dx, dc, i in steps + [(0, 1, RELAYED)]
     ]
+    start(second)
     for i in range(V_ONE, V_TWO):
         vz[i].wait_recv()
-        copies.append(forward(vrelay, vland, i))
+        vf[i].start()
     for copy in second:
         copy.wait()
     largest = maxes[2]
@@ -190,17 +208,15 @@
 
     lax.fori_loop(0, SEQS, scale_sequence, 0)
 
-    kz = [relay_out(narrow, krelay, i) for i in range(RELAYED)]
-    start(kz)
-    for dc in (0, 1):
-        copies.append(along_z(narrow, kland, dc))
+    kz, kf = relay_out(narrow, krelay), forward(krelay, kland)
+    straight = along_z(narrow, kland)
+    start(kz + straight)
     for i in range(V_TWO, RELAYED):
         vz[i].wait_recv()
-        copies.append(forward(vrelay, vland, i))
-    kx = [along_x(narrow, kland, i, 0, ROWS) for i in range(RELAYED)]
+        vf[i].start()
+    kx = along_x(narrow, kland, 0, ROWS) + to_sibling(narrow, kland)
     start(kx)
-    copies += kx
-    copies.append(to_sibling(narrow, kland))
+    copies += straight + kx + kf
 
     def keep_rows(c, _):
         kland[block(me, c * CHUNK, CHUNK), :] = narrow[
@@ -211,7 +227,7 @@
     lax.fori_loop(0, ROWS // CHUNK, keep_rows, 0)
     for i in range(RELAYED):
         kz[i].wait_recv()
-        copies.append(forward(krelay, kland, i))
+        kf[i].start()
     keep.wait()
     for copy in vz + kz:
         copy.wait_send()

time: 103 us -> 102 us (level)
    pallas_call x1, Pallas kernels: 98.8 us -> 97.3 us  [local(): pl.pallas_call(exchange, name='exchange', out_shape=(pltpu.VMEM((TOTAL, L...]
where the time goes in v4:
time: 102 us; the launch traced here: 101 us
  Pallas kernels  101 us (99%)
    pallas_call x1, Pallas kernels, local(): pl.pallas_call(exchange, name='exchange', out_shape=(pltpu.VMEM((TOTAL, L...  97.3 us
    pallas_call x1, Pallas kernels, local(): pl.pallas_call(store, name='store', out_shape=(jax.ShapeDtypeStruct((TOTA...  3.39 us

profile of v4, /device:TPU:1, one launch (start us, length us, event | category | flops | bytes accessed | tf_op | source)
XLA Modules:
  0.0 101.4 jit_solution(13128439879559698858)
XLA Ops:
  0.6 97.3 %exchange.1 = (bf16[16384,128]{1,0:T(8,128)(2,1)S(1)}, bf16[16384,128]{1,0:T(8,128)(2,1)S(1)}, f32[1,128]{1,0:T(1,128)S(1)}) custom-call(bf16[16,1024,128]{2,1,0:T(8,128)(2,1)} %bitcast.7, bf16[16,1024,128]{2,1,0:T(8,128)(2,1)} %bitcast.8, f32[64,16384]{1,0:T(8,128)} %bitcast.9, f32[1,128]{1,0:T(1,128)} %bitcast.10), custom_call_target="tpu_custom_call" | custom-call | tf_op jit(solution)/shard_map/exchange/pallas_call | solution.py:259
  98.0 3.4 %store.1 = (bf16[16384,128]{1,0:T(8,128)(2,1)}, bf16[16384,128]{1,0:T(8,128)(2,1)}, f32[1,128]{1,0:T(1,128)}) custom-call(bf16[16384,128]{1,0:T(8,128)(2,1)S(1)} %get-tuple-element.9.kland, bf16[16384,128]{1,0:T(8,128)(2,1)S(1)} %get-tuple-element.10.vland, f32[1,128]{1,0:T(1,128)S(1)} %get-tuple-element.11.scale), custom_call_target="tpu_custom_call" | custom-call | tf_op jit(solution)/shard_map/store/pallas_call | solution.py:299

commit v5 on v4

--- a/solution.py
+++ b/solution.py
@@ -17,18 +17,17 @@
 ALONG_X = (1, 3, 2)
 RELAYED = 2 * len(ALONG_X)
 PLANE = RELAYED + 1
-COPIES = 64
+ARRIVING = 15 * ROWS
 
 
 def exchange(
     keys, values, angle, gain,
     kland, vland, scale,
     raw, turned, narrow, krelay, vrelay, angles, gains_row, cosines, sines, maxes,
-    local_sem, ready_sem, send_sem, recv_sem,
+    local_sem, ready_sem, send_sem, land_sem, hop_sem, max_sem,
 ):
     far, near, model = lax.axis_index("farcp"), lax.axis_index("nearcp"), lax.axis_index("model")
     core, x, z = near % 2, ((near // 2) % 2) * 2 + far, near // 4
-    used = [0]
 
     def place(dx, dz, dc):
         px, pz, pc = (x + dx) % 4, (z + dz) % 2, (core + dc) % 2
@@ -49,19 +48,18 @@
     steps = [(dx, (core + to) % 2, n) for to in (1, 0) for n, dx in enumerate(ALONG_X)]
     steps = [(dx, dc, n + len(ALONG_X) * dc) for dx, dc, n in steps]
 
-    def plan(source, target, dx, dz, dc, slot):
+    def plan(source, target, dx, dz, dc, sent, arrived):
         return pltpu.make_async_remote_copy(
             src_ref=source,
             dst_ref=target,
-            send_sem=send_sem.at[slot],
-            recv_sem=recv_sem.at[slot],
+            send_sem=sent,
+            recv_sem=arrived,
             device_id=device(dx, dz, dc),
             device_id_type=MESH,
         )
 
-    def slots(count):
-        used[0] += count
-        return used[0] - count
+    def wait_for(ref, sem):
+        pltpu.make_async_copy(ref, ref, sem).wait()
 
     def start(copies):
         for copy in copies:
@@ -82,42 +80,48 @@
     pl.semaphore_wait(barrier, 3 + 4 * core)
     pl.semaphore_signal(ready_sem, inc=1, device_id=device(0, 0, 1), device_id_type=MESH)
 
-    def relay_out(source, relay):
-        base = slots(RELAYED)
-        return [
-            plan(source.at[index(dx, 1, dc)], relay.at[i], 0, 1, 0, base + i) for dx, dc, i in steps
-        ]
-
-    def forward(relay, land):
-        base = slots(RELAYED)
-        return [
-            plan(relay.at[i], land.at[block(across)], dx, 0, dc, base + i) for dx, dc, i in steps
-        ]
-
-    def along_x(source, land, first, rows):
-        base, part = slots(RELAYED), pl.ds(first, rows)
+    def relay_out(n, source, relay):
         return [
             plan(
-                source.at[index(dx, 0, dc), part],
-                land.at[block(me, first, rows)],
-                dx, 0, dc, base + i,
+                source.at[index(dx, 1, dc)], relay.at[i],
+                0, 1, 0, send_sem.at[n], hop_sem.at[n, i],
             )
             for dx, dc, i in steps
         ]
 
-    def along_z(source, land):
-        base = slots(2)
+    def forward(n, relay, land):
         return [
-            plan(source.at[index(0, 1, dc)], land.at[block(me)], 0, 1, dc, base + dc)
-            for dc in ((core + 1) % 2, core)
+            plan(
+                relay.at[i], land.at[block(across)],
+                dx, 0, dc, send_sem.at[2 + n], land_sem.at[n],
+            )
+            for dx, dc, i in steps
         ]
 
-    def to_sibling(source, land):
-        return [plan(source.at[index(0, 0, 1)], land.at[block(me)], 0, 0, 1, slots(1))]
-
-    vz, vf = relay_out(values, vrelay), forward(vrelay, vland)
-    vx = along_x(values, vland, 0, FIRST_ROWS)
-    side = to_sibling(values, vland)
+    def along_x(n, source, land, first, rows):
+        part = pl.ds(first, rows)
+        return [
+            plan(
+                source.at[index(dx, 0, dc), part], land.at[block(me, first, rows)],
+                dx, 0, dc, send_sem.at[2 + n], land_sem.at[n],
+            )
+            for dx, dc, i in steps
+        ]
+
+    def straight(n, source, land, dz, dc):
+        return plan(
+            source.at[index(0, dz, dc)], land.at[block(me)],
+            0, dz, dc, send_sem.at[2 + n], land_sem.at[n],
+        )
+
+    def along_z(n, source, land):
+        return [straight(n, source, land, 1, dc) for dc in ((core + 1) % 2, core)]
+
+    def to_sibling(n, source, land):
+        return [straight(n, source, land, 0, 1)]
+
+    vz, vf = relay_out(0, values, vrelay), forward(0, vrelay, vland)
+    vx = along_x(0, values, vland, 0, FIRST_ROWS)
 
     @pl.when(core == 0)
     def _():
@@ -137,8 +141,7 @@
     def _():
         start(vz[:Z_FIRST])
 
-    start(side)
-    copies = vx + vf + side
+    start(to_sibling(0, values, vland))
     keep.start()
 
     load_angles.wait()
@@ -170,29 +173,25 @@
 
     lax.fori_loop(0, SEQS, turn_sequence, 0)
 
-    first = plan(maxes.at[0], maxes.at[1], 0, 1, 0, slots(1))
+    first = plan(maxes.at[0], maxes.at[1], 0, 1, 0, max_sem.at[0], max_sem.at[1])
     first.start()
     start(vz[Z_FIRST:])
-    straight = along_z(values, vland)
-    rest = along_x(values, vland, FIRST_ROWS, ROWS - FIRST_ROWS)
-    start(straight + rest)
-    copies += straight + rest
+    start(along_z(0, values, vland))
+    start(along_x(0, values, vland, FIRST_ROWS, ROWS - FIRST_ROWS))
     for i in range(V_ONE):
         vz[i].wait_recv()
         vf[i].start()
     first.wait()
     maxes[2] = jnp.maximum(maxes[0], maxes[1])
-    base = slots(PLANE)
     second = [
-        plan(maxes.at[2], maxes.at[3 + i], dx, 0, dc, base + i)
+        plan(maxes.at[2], maxes.at[3 + i], dx, 0, dc, max_sem.at[2], max_sem.at[3])
         for dx, dc, i in steps + [(0, 1, RELAYED)]
     ]
     start(second)
     for i in range(V_ONE, V_TWO):
         vz[i].wait_recv()
         vf[i].start()
-    for copy in second:
-        copy.wait()
+    wait_for(maxes.at[pl.ds(3, PLANE)], max_sem.at[3])
     largest = maxes[2]
     for i in range(PLANE):
         largest = jnp.maximum(largest, maxes[3 + i])
@@ -208,15 +207,12 @@
 
     lax.fori_loop(0, SEQS, scale_sequence, 0)
 
-    kz, kf = relay_out(narrow, krelay), forward(krelay, kland)
-    straight = along_z(narrow, kland)
-    start(kz + straight)
+    kz, kf = relay_out(1, narrow, krelay), forward(1, krelay, kland)
+    start(kz + along_z(1, narrow, kland))
     for i in range(V_TWO, RELAYED):
         vz[i].wait_recv()
         vf[i].start()
-    kx = along_x(narrow, kland, 0, ROWS) + to_sibling(narrow, kland)
-    start(kx)
-    copies += straight + kx + kf
+    start(along_x(1, narrow, kland, 0, ROWS) + to_sibling(1, narrow, kland))
 
     def keep_rows(c, _):
         kland[block(me, c * CHUNK, CHUNK), :] = narrow[
@@ -229,10 +225,12 @@
         kz[i].wait_recv()
         kf[i].start()
     keep.wait()
-    for copy in vz + kz:
-        copy.wait_send()
-    for copy in copies:
-        copy.wait()
+    wait_for(maxes.at[pl.ds(3, PLANE)], max_sem.at[2])
+    for n, (relay, land) in enumerate(((vrelay, vland), (krelay, kland))):
+        arriving = land.at[pl.ds(0, ARRIVING)]
+        wait_for(relay, send_sem.at[n])
+        wait_for(arriving, send_sem.at[2 + n])
+        wait_for(arriving, land_sem.at[n])
 
 
 PIECES = 2
@@ -279,8 +277,10 @@
             pltpu.VMEM((3 + PLANE, SEQS, LANES), jnp.float32),
             pltpu.SemaphoreType.DMA((4,)),
             pltpu.SemaphoreType.REGULAR,
-            pltpu.SemaphoreType.DMA((COPIES,)),
-            pltpu.SemaphoreType.DMA((COPIES,)),
+            pltpu.SemaphoreType.DMA((4,)),
+            pltpu.SemaphoreType.DMA((2,)),
+            pltpu.SemaphoreType.DMA((2, RELAYED)),
+            pltpu.SemaphoreType.DMA((4,)),
         ],
         compiler_params=pltpu.CompilerParams(
             collective_id=0, has_side_effects=True, vmem_limit_bytes=40 * 2**20

time: 102 us -> 101 us (level)
  Pallas kernels: 101 us -> 99.7 us
where the time goes in v5:
time: 101 us; the launch traced here: 100 us
  Pallas kernels  99.7 us (99%)
    pallas_call x1, Pallas kernels, local(): pl.pallas_call(exchange, name='exchange', out_shape=(pltpu.VMEM((TOTAL, L...  96.3 us
    pallas_call x1, Pallas kernels, local(): pl.pallas_call(store, name='store', out_shape=(jax.ShapeDtypeStruct((TOTA...  3.39 us

profile of v5, /device:TPU:1, one launch (start us, length us, event | category | flops | bytes accessed | tf_op | source)
XLA Modules:
  0.0 100.4 jit_solution(17962580352334928578)
XLA Ops:
  0.6 96.3 %exchange.1 = (bf16[16384,128]{1,0:T(8,128)(2,1)S(1)}, bf16[16384,128]{1,0:T(8,128)(2,1)S(1)}, f32[1,128]{1,0:T(1,128)S(1)}) custom-call(bf16[16,1024,128]{2,1,0:T(8,128)(2,1)} %bitcast.7, bf16[16,1024,128]{2,1,0:T(8,128)(2,1)} %bitcast.8, f32[64,16384]{1,0:T(8,128)} %bitcast.9, f32[1,128]{1,0:T(1,128)} %bitcast.10), custom_call_target="tpu_custom_call" | custom-call | tf_op jit(solution)/shard_map/exchange/pallas_call | solution.py:257
  97.0 3.4 %store.1 = (bf16[16384,128]{1,0:T(8,128)(2,1)}, bf16[16384,128]{1,0:T(8,128)(2,1)}, f32[1,128]{1,0:T(1,128)}) custom-call(bf16[16384,128]{1,0:T(8,128)(2,1)S(1)} %get-tuple-element.9.kland, bf16[16384,128]{1,0:T(8,128)(2,1)S(1)} %get-tuple-element.10.vland, f32[1,128]{1,0:T(1,128)S(1)} %get-tuple-element.11.scale), custom_call_target="tpu_custom_call" | custom-call | tf_op jit(solution)/shard_map/store/pallas_call | solution.py:299

commit v6 on v5

--- a/solution.py
+++ b/solution.py
@@ -9,9 +9,9 @@
 SEQS, ROWS, LANES, HALF = 16, 1024, 128, 64
 TOTAL = SEQS * ROWS
 CHUNK = 128
-FIRST_ROWS = 768
-Z_FIRST = 3
-V_ONE, V_TWO = 2, 4
+FIRST_ROWS = 896
+Z_FIRST = 4
+V_ONE, V_TWO = 3, 6
 
 
 ALONG_X = (1, 3, 2)
@@ -27,11 +27,11 @@
     local_sem, ready_sem, send_sem, land_sem, hop_sem, max_sem,
 ):
     far, near, model = lax.axis_index("farcp"), lax.axis_index("nearcp"), lax.axis_index("model")
-    core, x, z = near % 2, ((near // 2) % 2) * 2 + far, near // 4
+    core, x, z = lax.rem(near, 2), lax.rem(lax.div(near, 2), 2) * 2 + far, lax.div(near, 4)
 
     def place(dx, dz, dc):
-        px, pz, pc = (x + dx) % 4, (z + dz) % 2, (core + dc) % 2
-        return px % 2, pz * 4 + (px // 2) * 2 + pc
+        px, pz, pc = lax.rem(x + dx, 4), lax.rem(z + dz, 2), lax.rem(core + dc, 2)
+        return lax.rem(px, 2), pz * 4 + lax.div(px, 2) * 2 + pc
 
     def device(dx, dz, dc):
         return (*place(dx, dz, dc), model)
@@ -45,7 +45,7 @@
 
     me, across = far * 8 + near, index(0, 1, 0)
 
-    steps = [(dx, (core + to) % 2, n) for to in (1, 0) for n, dx in enumerate(ALONG_X)]
+    steps = [(dx, lax.rem(core + to, 2), n) for to in (1, 0) for n, dx in enumerate(ALONG_X)]
     steps = [(dx, dc, n + len(ALONG_X) * dc) for dx, dc, n in steps]
 
     def plan(source, target, dx, dz, dc, sent, arrived):
@@ -115,7 +115,7 @@
         )
 
     def along_z(n, source, land):
-        return [straight(n, source, land, 1, dc) for dc in ((core + 1) % 2, core)]
+        return [straight(n, source, land, 1, dc) for dc in (1 - core, core)]
 
     def to_sibling(n, source, land):
         return [straight(n, source, land, 0, 1)]

time: 101 us -> 101 us (level)
  no operation moved by 1% of the time
where the time goes in v6:
time: 101 us; the launch traced here: 100 us
  Pallas kernels  99.7 us (99%)
    pallas_call x1, Pallas kernels, local(): pl.pallas_call(exchange, name='exchange', out_shape=(pltpu.VMEM((TOTAL, L...  96.3 us
    pallas_call x1, Pallas kernels, local(): pl.pallas_call(store, name='store', out_shape=(jax.ShapeDtypeStruct((TOTA...  3.39 us

profile of v6, /device:TPU:1, one launch (start us, length us, event | category | flops | bytes accessed | tf_op | source)
XLA Modules:
  0.0 100.4 jit_solution(8470873110883904764)
XLA Ops:
  0.6 96.3 %exchange.1 = (bf16[16384,128]{1,0:T(8,128)(2,1)S(1)}, bf16[16384,128]{1,0:T(8,128)(2,1)S(1)}, f32[1,128]{1,0:T(1,128)S(1)}) custom-call(bf16[16,1024,128]{2,1,0:T(8,128)(2,1)} %bitcast.7, bf16[16,1024,128]{2,1,0:T(8,128)(2,1)} %bitcast.8, f32[64,16384]{1,0:T(8,128)} %bitcast.9, f32[1,128]{1,0:T(1,128)} %bitcast.10), custom_call_target="tpu_custom_call" | custom-call | tf_op jit(solution)/shard_map/exchange/pallas_call | solution.py:257
  97.0 3.4 %store.1 = (bf16[16384,128]{1,0:T(8,128)(2,1)}, bf16[16384,128]{1,0:T(8,128)(2,1)}, f32[1,128]{1,0:T(1,128)}) custom-call(bf16[16384,128]{1,0:T(8,128)(2,1)S(1)} %get-tuple-element.9.kland, bf16[16384,128]{1,0:T(8,128)(2,1)S(1)} %get-tuple-element.10.vland, f32[1,128]{1,0:T(1,128)S(1)} %get-tuple-element.11.scale), custom_call_target="tpu_custom_call" | custom-call | tf_op jit(solution)/shard_map/store/pallas_call | solution.py:299

commit v7 on v6

--- a/solution.py
+++ b/solution.py
@@ -84,7 +84,7 @@
         return [
             plan(
                 source.at[index(dx, 1, dc)], relay.at[i],
-                0, 1, 0, send_sem.at[n], hop_sem.at[n, i],
+                0, 1, 0, send_sem.at[0], hop_sem.at[n, i],
             )
             for dx, dc, i in steps
         ]
@@ -93,7 +93,7 @@
         return [
             plan(
                 relay.at[i], land.at[block(across)],
-                dx, 0, dc, send_sem.at[2 + n], land_sem.at[n],
+                dx, 0, dc, send_sem.at[1], land_sem.at[0],
             )
             for dx, dc, i in steps
         ]
@@ -103,7 +103,7 @@
         return [
             plan(
                 source.at[index(dx, 0, dc), part], land.at[block(me, first, rows)],
-                dx, 0, dc, send_sem.at[2 + n], land_sem.at[n],
+                dx, 0, dc, send_sem.at[1], land_sem.at[0],
             )
             for dx, dc, i in steps
         ]
@@ -111,7 +111,7 @@
     def straight(n, source, land, dz, dc):
         return plan(
             source.at[index(0, dz, dc)], land.at[block(me)],
-            0, dz, dc, send_sem.at[2 + n], land_sem.at[n],
+            0, dz, dc, send_sem.at[1], land_sem.at[0],
         )
 
     def along_z(n, source, land):
@@ -226,11 +226,9 @@
         kf[i].start()
     keep.wait()
     wait_for(maxes.at[pl.ds(3, PLANE)], max_sem.at[2])
-    for n, (relay, land) in enumerate(((vrelay, vland), (krelay, kland))):
-        arriving = land.at[pl.ds(0, ARRIVING)]
-        wait_for(relay, send_sem.at[n])
-        wait_for(arriving, send_sem.at[2 + n])
-        wait_for(arriving, land_sem.at[n])
+    wait_for(turned.at[pl.ds(0, RELAYED)], send_sem.at[0])
+    wait_for(turned.at[pl.ds(0, 15)], send_sem.at[1])
+    wait_for(turned.at[pl.ds(0, 15)], land_sem.at[0])
 
 
 PIECES = 2
@@ -277,8 +275,8 @@
             pltpu.VMEM((3 + PLANE, SEQS, LANES), jnp.float32),
             pltpu.SemaphoreType.DMA((4,)),
             pltpu.SemaphoreType.REGULAR,
-            pltpu.SemaphoreType.DMA((4,)),
             pltpu.SemaphoreType.DMA((2,)),
+            pltpu.SemaphoreType.DMA((1,)),
             pltpu.SemaphoreType.DMA((2, RELAYED)),
             pltpu.SemaphoreType.DMA((4,)),
         ],

time: 101 us -> 101 us (level)
  no operation moved by 1% of the time
where the time goes in v7:
time: 101 us; the launch traced here: 100 us
  Pallas kernels  99.7 us (99%)
    pallas_call x1, Pallas kernels, local(): pl.pallas_call(exchange, name='exchange', out_shape=(pltpu.VMEM((TOTAL, L...  96.3 us
    pallas_call x1, Pallas kernels, local(): pl.pallas_call(store, name='store', out_shape=(jax.ShapeDtypeStruct((TOTA...  3.39 us

profile of v7, /device:TPU:1, one launch (start us, length us, event | category | flops | bytes accessed | tf_op | source)
XLA Modules:
  0.0 100.3 jit_solution(9705615195803885726)
XLA Ops:
  0.6 96.3 %exchange.1 = (bf16[16384,128]{1,0:T(8,128)(2,1)S(1)}, bf16[16384,128]{1,0:T(8,128)(2,1)S(1)}, f32[1,128]{1,0:T(1,128)S(1)}) custom-call(bf16[16,1024,128]{2,1,0:T(8,128)(2,1)} %bitcast.7, bf16[16,1024,128]{2,1,0:T(8,128)(2,1)} %bitcast.8, f32[64,16384]{1,0:T(8,128)} %bitcast.9, f32[1,128]{1,0:T(1,128)} %bitcast.10), custom_call_target="tpu_custom_call" | custom-call | tf_op jit(solution)/shard_map/exchange/pallas_call | solution.py:255
  96.9 3.4 %store.1 = (bf16[16384,128]{1,0:T(8,128)(2,1)}, bf16[16384,128]{1,0:T(8,128)(2,1)}, f32[1,128]{1,0:T(1,128)}) custom-call(bf16[16384,128]{1,0:T(8,128)(2,1)S(1)} %get-tuple-element.9.kland, bf16[16384,128]{1,0:T(8,128)(2,1)S(1)} %get-tuple-element.10.vland, f32[1,128]{1,0:T(1,128)S(1)} %get-tuple-element.11.scale), custom_call_target="tpu_custom_call" | custom-call | tf_op jit(solution)/shard_map/store/pallas_call | solution.py:297

commit v8 on v6

--- a/solution.py
+++ b/solution.py
@@ -45,7 +45,8 @@
 
     me, across = far * 8 + near, index(0, 1, 0)
 
-    steps = [(dx, lax.rem(core + to, 2), n) for to in (1, 0) for n, dx in enumerate(ALONG_X)]
+    turns = ((1, (0, 1, 2)), (0, (2, 0, 1)))
+    steps = [(ALONG_X[n], lax.rem(core + to, 2), n) for to, order in turns for n in order]
     steps = [(dx, dc, n + len(ALONG_X) * dc) for dx, dc, n in steps]
 
     def plan(source, target, dx, dz, dc, sent, arrived):

time: 101 us -> 101 us (level)
  no operation moved by 1% of the time
where the time goes in v8:
time: 101 us; the launch traced here: 100 us
  Pallas kernels  99.7 us (99%)
    pallas_call x1, Pallas kernels, local(): pl.pallas_call(exchange, name='exchange', out_shape=(pltpu.VMEM((TOTAL, L...  96.3 us
    pallas_call x1, Pallas kernels, local(): pl.pallas_call(store, name='store', out_shape=(jax.ShapeDtypeStruct((TOTA...  3.39 us

profile of v8, /device:TPU:1, one launch (start us, length us, event | category | flops | bytes accessed | tf_op | source)
XLA Modules:
  0.0 100.4 jit_solution(13669421410400691130)
XLA Ops:
  0.6 96.3 %exchange.1 = (bf16[16384,128]{1,0:T(8,128)(2,1)S(1)}, bf16[16384,128]{1,0:T(8,128)(2,1)S(1)}, f32[1,128]{1,0:T(1,128)S(1)}) custom-call(bf16[16,1024,128]{2,1,0:T(8,128)(2,1)} %bitcast.7, bf16[16,1024,128]{2,1,0:T(8,128)(2,1)} %bitcast.8, f32[64,16384]{1,0:T(8,128)} %bitcast.9, f32[1,128]{1,0:T(1,128)} %bitcast.10), custom_call_target="tpu_custom_call" | custom-call | tf_op jit(solution)/shard_map/exchange/pallas_call | solution.py:258
  97.0 3.4 %store.1 = (bf16[16384,128]{1,0:T(8,128)(2,1)}, bf16[16384,128]{1,0:T(8,128)(2,1)}, f32[1,128]{1,0:T(1,128)}) custom-call(bf16[16384,128]{1,0:T(8,128)(2,1)S(1)} %get-tuple-element.9.kland, bf16[16384,128]{1,0:T(8,128)(2,1)S(1)} %get-tuple-element.10.vland, f32[1,128]{1,0:T(1,128)S(1)} %get-tuple-element.11.scale), custom_call_target="tpu_custom_call" | custom-call | tf_op jit(solution)/shard_map/store/pallas_call | solution.py:300
